TPU v7x, 32 devices: a whole 2x2x4 slice. The times are simulated.
32 devices in a mesh: ctx: 8 (over z, core), tp: 4 (over y, x).
Axes of the slice: x: 2, y: 2, z: 4, core: 2. Of those that a mesh axis runs over, the one named last changes fastest.
Arguments:
- tokens: bfloat16 [2, 4096, 8192], P(None, 'ctx', 'tp'), may hold values from -14 to 14
- norm_gain: float32 [8192], replicated, may hold values from 0.5 to 1.5
- span_order: int32 [2, 16], replicated, may hold values from 0 to 15, each once within a row
- w_query: bfloat16 [8192, 4096], P('ctx', 'tp'), may hold values from -0.10122281 to 0.10122281
- w_key: bfloat16 [8192, 1024], P('ctx', 'tp'), may hold values from -0.10122281 to 0.10122281
- value_weight: bfloat16 [8192, 1024], P('ctx', 'tp'), may hold values from -0.0625 to 0.0625
- w_out: bfloat16 [4096, 8192], P('tp', 'ctx'), may hold values from -0.75 to 0.75
Outputs:
- mixed: bfloat16 [2, 4096, 8192], P(None, 'ctx', 'tp')
Inputs may be any that keep to these rules, and one draw needn't show every extreme that they name: Each row of span_order names every one of the 2 * 8 blocks of positions once; stored block b of a sequence holds positions span_order[b] * 256 onwards, in order.
All inputs are finite; a program needn't handle non-finite values.
Results may differ from a plain program's by a relative error of at most 0.014.
Values may be sent and summed in bfloat16 or wider, within the bound.
A program may use at most 128 MiB of HBM per device.

v0:
```python
import math
import jax
import jax.numpy as jnp
from jax import lax
from jax.sharding import PartitionSpec as P

HEAD_DIM = 128
theta_base = 500000.0
norm_eps = 1e-05
masked_score = -1e30


def normalize(flat_rows, norm_gain):
    wide = flat_rows.astype(jnp.float32)
    factor = lax.rsqrt(jnp.mean(wide * wide, axis=-1, keepdims=True) + norm_eps)
    return (wide * factor * norm_gain).astype(jnp.bfloat16)


def positions_of(span_order, first, count, block_rows):
    stored = first + jnp.arange(count, dtype=jnp.int32)
    which = stored // block_rows
    slots = jnp.arange(span_order.shape[1], dtype=jnp.int32)
    picked = jnp.sum(
        jnp.where(slots[None, None, :] == which[None, :, None], span_order[:, None, :], 0), axis=2
    )
    return picked * block_rows + stored % block_rows


def apply_rotation(value_rows, token_position, head_size):
    half = head_size // 2
    freqs = jnp.exp(-(2.0 * jnp.arange(half, dtype=jnp.float32) / head_size) * math.log(theta_base))
    angle = token_position.astype(jnp.float32)[..., None] * freqs
    cosine = jnp.cos(angle)[:, :, None, :]
    sine = jnp.sin(angle)[:, :, None, :]
    front = value_rows[..., :half]
    back = value_rows[..., half:]
    return jnp.concatenate([front * cosine - back * sine, back * cosine + front * sine], axis=-1)


def per_device(tokens, norm_gain, span_order, w_query, w_key, value_weight, w_out):
    sequence_batch, rows_dev, _ = tokens.shape
    head_size = HEAD_DIM
    query_heads = w_query.shape[1] // head_size
    key_heads = w_key.shape[1] // head_size
    group_width = query_heads // key_heads
    block_rows = rows_dev // 2
    total_rows = sequence_batch * rows_dev
    factor = 1.0 / math.sqrt(head_size)
    rank = lax.axis_index("ctx")
    whole = lax.all_gather(tokens, "tp", axis=2, tiled=True)
    normed = normalize(whole.reshape(total_rows, whole.shape[2]), norm_gain)
    query_pos = positions_of(span_order, rank * rows_dev, rows_dev, block_rows)
    latest = jnp.max(query_pos, axis=1)
    stat_shape = (sequence_batch, key_heads, group_width, rows_dev)
    initial = (
        jnp.full(stat_shape, masked_score, jnp.float32),
        jnp.zeros(stat_shape, jnp.float32),
        jnp.zeros(stat_shape + (head_size,), jnp.float32),
    )
    pieces = (
        lax.all_gather(w_query, "ctx", axis=0, tiled=True),
        lax.all_gather(w_key, "ctx", axis=0, tiled=True),
        lax.all_gather(value_weight, "ctx", axis=0, tiled=True),
    )
    query_flat, flattened_key, flattened_value = tuple(
        (jnp.dot(normed, piece, preferred_element_type=jnp.float32) for piece in pieces)
    )
    turned = apply_rotation(
        query_flat.reshape(sequence_batch, rows_dev, query_heads, head_size), query_pos, head_size
    ).astype(jnp.bfloat16)
    query = turned.reshape(sequence_batch, rows_dev, key_heads, group_width, head_size).transpose(
        0, 2, 3, 1, 4
    )
    turned = apply_rotation(
        flattened_key.reshape(sequence_batch, rows_dev, key_heads, head_size), query_pos, head_size
    ).astype(jnp.bfloat16)
    own_values = flattened_value.reshape(sequence_batch, rows_dev, key_heads, head_size).astype(
        jnp.bfloat16
    )
    key_piece = lax.all_gather(turned, "ctx", axis=1, tiled=True)
    value_piece = lax.all_gather(own_values, "ctx", axis=1, tiled=True)
    count = key_piece.shape[1]
    step_rows = 512

    def one_block(index, state):
        first = index * step_rows
        key_block = lax.dynamic_slice_in_dim(key_piece, first, step_rows, 1)
        value_block = lax.dynamic_slice_in_dim(value_piece, first, step_rows, 1)
        key_pos = positions_of(span_order, first, step_rows, block_rows)

        def update(current):
            peak, total, summed = current
            scores = (
                jnp.einsum(
                    "shgqd,skhd->shgqk", query, key_block, preferred_element_type=jnp.float32
                )
                * factor
            )
            allowed = key_pos[:, None, None, None, :] <= query_pos[:, None, None, :, None]
            scores = jnp.where(allowed, scores, masked_score)
            new_peak = jnp.maximum(peak, jnp.max(scores, axis=-1))
            weights = jnp.where(allowed, jnp.exp(scores - new_peak[..., None]), 0.0)
            shrink = jnp.exp(peak - new_peak)
            total = total * shrink + jnp.sum(weights, axis=-1)
            summed = summed * shrink[..., None] + jnp.einsum(
                "shgqk,skhd->shgqd",
                weights.astype(jnp.bfloat16),
                value_block,
                preferred_element_type=jnp.float32,
            )
            return (new_peak, total, summed)

        return lax.cond(
            jnp.all(jnp.min(key_pos, axis=1) > latest), lambda kept: kept, update, state
        )

    peak, total, summed = lax.fori_loop(0, count // step_rows, one_block, initial)
    attended = (summed / total[..., None]).astype(jnp.bfloat16)
    attended = attended.transpose(0, 3, 1, 2, 4).reshape(total_rows, query_heads * head_size)
    terms = jnp.dot(
        attended,
        lax.all_gather(w_out, "ctx", axis=1, tiled=True),
        preferred_element_type=jnp.float32,
    )
    mixed = lax.psum_scatter(terms.astype(jnp.bfloat16), "tp", scatter_dimension=1, tiled=True)
    return mixed.reshape(sequence_batch, rows_dev, mixed.shape[1])


def solution(mesh):
    placed = (
        P(None, "ctx", "tp"),
        P(),
        P(),
        P("ctx", "tp"),
        P("ctx", "tp"),
        P("ctx", "tp"),
        P("tp", "ctx"),
    )
    return jax.shard_map(
        per_device, mesh=mesh, in_specs=placed, out_specs=P(None, "ctx", "tp"), check_vma=False
    )
```

profile of v0, /device:TPU:0, one launch (start us, length us, event | category | flops | bytes accessed | tf_op | source)
XLA Modules:
  0.0 862.1 jit_solution(7252307660646929625)
XLA Ops:
  10.5 48.0 %all-gather.10.cloned.1.call-done = bf16[8192,256]{1,0:T(8,128)(2,1)} async-done(((bf16[1024,256]{1,0:T(8,128)(2,1)}), bf16[8192,256]{1,0:T(8,128)(2,1)}) %all-gather.10.cloned.1.call-update) | async-done | bytes 4194320 | tf_op jit(solution)/shard_map/all_gather | solution.py:62
  58.6 6.3 copy.24
  64.9 151.7 %all-gather.8.cloned.1.call-done = bf16[2,512,8192]{2,1,0:T(8,128)(2,1)} async-done(((bf16[2,512,2048]{2,1,0:T(8,128)(2,1)}), bf16[2,512,8192]{2,1,0:T(8,128)(2,1)}) %all-gather.8.cloned.1.call-update) | async-done | bytes 16777232 | tf_op jit(solution)/shard_map/all_gather | solution.py:50
  216.5 7.5 fusion.21
  224.0 9.0 %fusion.29 = f32[2,512,2,128]{1,3,2,0:T(8,128)S(1)} fusion(bf16[2,128,8192,1]{2,1,0,3:T(8,128)(2,1)S(1)} %bitcast.69, bf16[2,512,8192]{2,1,0:T(8,128)(2,1)} %all-gather.8.cloned.1.call-done, f32[8192]{0:T(1024)S(1)} %copy-done.2, f32[2,512]{1,0:T(2,128)S(1)} %add_rsqrt_fusion), kind=kOutput, calls=%fused_computation.49 | convolution fusion | flops 4328521728 | bytes 22056960 | tf_op jit(solution)/shard_map/dot_general | solution.py:66
  234.2 30.9 %all-gather.16.cloned.1.call-done = bf16[8192,256]{1,0:T(8,128)(2,1)} async-done(((bf16[1024,256]{1,0:T(8,128)(2,1)}), bf16[8192,256]{1,0:T(8,128)(2,1)}) %all-gather.16.cloned.1.call-update) | async-done | bytes 4194320 | tf_op jit(solution)/shard_map/all_gather | solution.py:63
  265.1 6.3 copy.28
  271.4 12.7 %convolution_convert_fusion.1 = bf16[2,512,2,128]{3,1,2,0:T(8,128)(2,1)} fusion(bf16[2,128,8192,1]{2,1,0,3:T(8,128)(2,1)} %bitcast.70, bf16[2,512,8192]{2,1,0:T(8,128)(2,1)} %all-gather.8.cloned.1.call-done, f32[8192]{0:T(1024)S(1)} %copy-done.2, f32[2,512]{1,0:T(2,128)S(1)} %add_rsqrt_fusion), kind=kOutput, calls=%fused_computation.47 | convolution fusion | flops 4328783872 | bytes 21532672 | tf_op jit(solution)/shard_map/dot_general | solution.py:66
  285.2 131.2 %all-gather.14.cloned.1.call-done = bf16[8192,1024]{1,0:T(8,128)(2,1)} async-done(((bf16[1024,1024]{1,0:T(8,128)(2,1)}), bf16[8192,1024]{1,0:T(8,128)(2,1)}) %all-gather.14.cloned.1.call-update) | async-done | bytes 16777232 | tf_op jit(solution)/shard_map/all_gather | solution.py:61
  416.4 21.4 %copy.25 = bf16[1024,8192]{1,0:T(8,128)(2,1)} copy(bf16[1024,8192]{0,1:T(8,128)(2,1)} %bitcast.63) | data formatting | bytes 33554432 | tf_op jit(solution)/shard_map/dot_general | solution.py:66
  437.9 22.4 %fusion.27 = f32[2,512,8,128]{1,3,2,0:T(8,128)S(1)} fusion(bf16[8,128,8192,1]{2,1,0,3:T(8,128)(2,1)} %bitcast.64, bf16[2,512,8192]{2,1,0:T(8,128)(2,1)} %all-gather.8.cloned.1.call-done, f32[8192]{0:T(1024)S(1)} %copy-done.2, f32[2,512]{1,0:T(2,128)S(1)} %add_rsqrt_fusion), kind=kOutput, calls=%fused_computation.48 | convolution fusion | flops 17213423616 | bytes 37785600 | tf_op jit(solution)/shard_map/dot_general | solution.py:66
  469.9 6.4 copy.29
  476.3 33.8 %all-gather.18.cloned.1.call-done = bf16[2,4096,2,128]{3,1,2,0:T(8,128)(2,1)} async-done(((bf16[2,512,2,128]{3,1,2,0:T(8,128)(2,1)}), bf16[2,4096,2,128]{3,1,2,0:T(8,128)(2,1)}) %all-gather.18.cloned.1.call-update) | async-done | bytes 4194320 | tf_op jit(solution)/shard_map/all_gather | solution.py:81
  512.6 156.1 %while.19 = (s32[]{:T(128)}, f32[2,2,4,512]{3,2,1,0:T(4,128)S(1)}, f32[2,2,4,512]{3,2,1,0:T(4,128)S(1)}, f32[2,2,4,512,128]{4,3,2,1,0:T(8,128)}, s32[2,16]{1,0:T...) while((s32[]{:T(128)}, f32[2,2,4,512]{3,2,1,0:T(4,128)S(1)}, ...), condition=%wide.region_11.12_spmd, body=%wide.region_3.11_spmd.sunk | while | flops 2204700672 | bytes 64532936 | solution.py:117
  514.2 17.9 %conditional.2 = (f32[2,2,4,512]{3,2,1,0:T(4,128)S(1)}, f32[2,2,4,512]{3,2,1,0:T(4,128)S(1)}, f32[2,2,4,512,128]{4,3,2,1,0:T(8,128)}) conditional(s32[]{:T(128)} %convert_element_type.85, (s32[2,512]{1,0:T(2,128)S(1)}, s32[2,512]{1,0:T(2,128)S(1)}, s32[]{:T(128)}, bf16[2,4096,2,128]{3,1,2,0:T(8,128)(2,1)}, bf16[2,2,4,512,128]{4,3,2,1,0:T(8,128)(2,1)}, ...), branch_computations={%region_7.9_spmd, %region_10.10_spmd} | conditional | flops 2204647424 | bytes 64430148 | solution.py:113
  523.5 8.7 %multiply_add_fusion = f32[2,2,4,512,128]{4,3,2,1,0:T(8,128)} fusion(f32[2,2,4,512,128]{4,3,2,1,0:T(8,128)} %get-tuple-element.360, f32[2,2,4,512]{3,2,1,0:T(4,128)S(1)} %bitcast.76, f32[2,2,512,4,512]{4,2,3,1,0:T(8,128)S(1)} %get-tuple-element.437, f32[2,2,4,512]{3,2,1,0:T(4,128)S(1)} %max.5, pred[2,512,512]{1,2,0:T(8,128)(4,1)S(1)} %broadcast_compare_fusion, ...), kind=kOutput, calls=%fused_computation.7 | convolution fusion | flops 1096810496 | bytes 26279940 | tf_op jit(solution)/shard_map/while/body/eval_jaxpr/cond/branch_0_fun/shgqk,skhd->shgqd/dot_general | solution.py:105
  533.8 17.9 %conditional.2 = (f32[2,2,4,512]{3,2,1,0:T(4,128)S(1)}, f32[2,2,4,512]{3,2,1,0:T(4,128)S(1)}, f32[2,2,4,512,128]{4,3,2,1,0:T(8,128)}) conditional(s32[]{:T(128)} %convert_element_type.85, (s32[2,512]{1,0:T(2,128)S(1)}, s32[2,512]{1,0:T(2,128)S(1)}, s32[]{:T(128)}, bf16[2,4096,2,128]{3,1,2,0:T(8,128)(2,1)}, bf16[2,2,4,512,128]{4,3,2,1,0:T(8,128)(2,1)}, ...), branch_computations={%region_7.9_spmd, %region_10.10_spmd} | conditional | flops 2204647424 | bytes 64430148 | solution.py:113
  543.0 8.7 %multiply_add_fusion = f32[2,2,4,512,128]{4,3,2,1,0:T(8,128)} fusion(f32[2,2,4,512,128]{4,3,2,1,0:T(8,128)} %get-tuple-element.360, f32[2,2,4,512]{3,2,1,0:T(4,128)S(1)} %bitcast.76, f32[2,2,512,4,512]{4,2,3,1,0:T(8,128)S(1)} %get-tuple-element.437, f32[2,2,4,512]{3,2,1,0:T(4,128)S(1)} %max.5, pred[2,512,512]{1,2,0:T(8,128)(4,1)S(1)} %broadcast_compare_fusion, ...), kind=kOutput, calls=%fused_computation.7 | convolution fusion | flops 1096810496 | bytes 26279940 | tf_op jit(solution)/shard_map/while/body/eval_jaxpr/cond/branch_0_fun/shgqk,skhd->shgqd/dot_general | solution.py:105
  553.3 17.9 %conditional.2 = (f32[2,2,4,512]{3,2,1,0:T(4,128)S(1)}, f32[2,2,4,512]{3,2,1,0:T(4,128)S(1)}, f32[2,2,4,512,128]{4,3,2,1,0:T(8,128)}) conditional(s32[]{:T(128)} %convert_element_type.85, (s32[2,512]{1,0:T(2,128)S(1)}, s32[2,512]{1,0:T(2,128)S(1)}, s32[]{:T(128)}, bf16[2,4096,2,128]{3,1,2,0:T(8,128)(2,1)}, bf16[2,2,4,512,128]{4,3,2,1,0:T(8,128)(2,1)}, ...), branch_computations={%region_7.9_spmd, %region_10.10_spmd} | conditional | flops 2204647424 | bytes 64430148 | solution.py:113
  562.5 8.7 %multiply_add_fusion = f32[2,2,4,512,128]{4,3,2,1,0:T(8,128)} fusion(f32[2,2,4,512,128]{4,3,2,1,0:T(8,128)} %get-tuple-element.360, f32[2,2,4,512]{3,2,1,0:T(4,128)S(1)} %bitcast.76, f32[2,2,512,4,512]{4,2,3,1,0:T(8,128)S(1)} %get-tuple-element.437, f32[2,2,4,512]{3,2,1,0:T(4,128)S(1)} %max.5, pred[2,512,512]{1,2,0:T(8,128)(4,1)S(1)} %broadcast_compare_fusion, ...), kind=kOutput, calls=%fused_computation.7 | convolution fusion | flops 1096810496 | bytes 26279940 | tf_op jit(solution)/shard_map/while/body/eval_jaxpr/cond/branch_0_fun/shgqk,skhd->shgqd/dot_general | solution.py:105
  572.8 17.9 %conditional.2 = (f32[2,2,4,512]{3,2,1,0:T(4,128)S(1)}, f32[2,2,4,512]{3,2,1,0:T(4,128)S(1)}, f32[2,2,4,512,128]{4,3,2,1,0:T(8,128)}) conditional(s32[]{:T(128)} %convert_element_type.85, (s32[2,512]{1,0:T(2,128)S(1)}, s32[2,512]{1,0:T(2,128)S(1)}, s32[]{:T(128)}, bf16[2,4096,2,128]{3,1,2,0:T(8,128)(2,1)}, bf16[2,2,4,512,128]{4,3,2,1,0:T(8,128)(2,1)}, ...), branch_computations={%region_7.9_spmd, %region_10.10_spmd} | conditional | flops 2204647424 | bytes 64430148 | solution.py:113
  582.0 8.7 %multiply_add_fusion = f32[2,2,4,512,128]{4,3,2,1,0:T(8,128)} fusion(f32[2,2,4,512,128]{4,3,2,1,0:T(8,128)} %get-tuple-element.360, f32[2,2,4,512]{3,2,1,0:T(4,128)S(1)} %bitcast.76, f32[2,2,512,4,512]{4,2,3,1,0:T(8,128)S(1)} %get-tuple-element.437, f32[2,2,4,512]{3,2,1,0:T(4,128)S(1)} %max.5, pred[2,512,512]{1,2,0:T(8,128)(4,1)S(1)} %broadcast_compare_fusion, ...), kind=kOutput, calls=%fused_computation.7 | convolution fusion | flops 1096810496 | bytes 26279940 | tf_op jit(solution)/shard_map/while/body/eval_jaxpr/cond/branch_0_fun/shgqk,skhd->shgqd/dot_general | solution.py:105
  592.3 17.9 %conditional.2 = (f32[2,2,4,512]{3,2,1,0:T(4,128)S(1)}, f32[2,2,4,512]{3,2,1,0:T(4,128)S(1)}, f32[2,2,4,512,128]{4,3,2,1,0:T(8,128)}) conditional(s32[]{:T(128)} %convert_element_type.85, (s32[2,512]{1,0:T(2,128)S(1)}, s32[2,512]{1,0:T(2,128)S(1)}, s32[]{:T(128)}, bf16[2,4096,2,128]{3,1,2,0:T(8,128)(2,1)}, bf16[2,2,4,512,128]{4,3,2,1,0:T(8,128)(2,1)}, ...), branch_computations={%region_7.9_spmd, %region_10.10_spmd} | conditional | flops 2204647424 | bytes 64430148 | solution.py:113
  601.7 8.6 multiply_add_fusion
  611.9 17.8 %conditional.2 = (f32[2,2,4,512]{3,2,1,0:T(4,128)S(1)}, f32[2,2,4,512]{3,2,1,0:T(4,128)S(1)}, f32[2,2,4,512,128]{4,3,2,1,0:T(8,128)}) conditional(s32[]{:T(128)} %convert_element_type.85, (s32[2,512]{1,0:T(2,128)S(1)}, s32[2,512]{1,0:T(2,128)S(1)}, s32[]{:T(128)}, bf16[2,4096,2,128]{3,1,2,0:T(8,128)(2,1)}, bf16[2,2,4,512,128]{4,3,2,1,0:T(8,128)(2,1)}, ...), branch_computations={%region_7.9_spmd, %region_10.10_spmd} | conditional | flops 2204647424 | bytes 64430148 | solution.py:113
  621.1 8.6 multiply_add_fusion
  631.4 17.8 %conditional.2 = (f32[2,2,4,512]{3,2,1,0:T(4,128)S(1)}, f32[2,2,4,512]{3,2,1,0:T(4,128)S(1)}, f32[2,2,4,512,128]{4,3,2,1,0:T(8,128)}) conditional(s32[]{:T(128)} %convert_element_type.85, (s32[2,512]{1,0:T(2,128)S(1)}, s32[2,512]{1,0:T(2,128)S(1)}, s32[]{:T(128)}, bf16[2,4096,2,128]{3,1,2,0:T(8,128)(2,1)}, bf16[2,2,4,512,128]{4,3,2,1,0:T(8,128)(2,1)}, ...), branch_computations={%region_7.9_spmd, %region_10.10_spmd} | conditional | flops 2204647424 | bytes 64430148 | solution.py:113
  640.6 8.6 multiply_add_fusion
  650.8 17.9 %conditional.2 = (f32[2,2,4,512]{3,2,1,0:T(4,128)S(1)}, f32[2,2,4,512]{3,2,1,0:T(4,128)S(1)}, f32[2,2,4,512,128]{4,3,2,1,0:T(8,128)}) conditional(s32[]{:T(128)} %convert_element_type.85, (s32[2,512]{1,0:T(2,128)S(1)}, s32[2,512]{1,0:T(2,128)S(1)}, s32[]{:T(128)}, bf16[2,4096,2,128]{3,1,2,0:T(8,128)(2,1)}, bf16[2,2,4,512,128]{4,3,2,1,0:T(8,128)(2,1)}, ...), branch_computations={%region_7.9_spmd, %region_10.10_spmd} | conditional | flops 2204647424 | bytes 64430148 | solution.py:113
  660.0 8.7 %multiply_add_fusion = f32[2,2,4,512,128]{4,3,2,1,0:T(8,128)} fusion(f32[2,2,4,512,128]{4,3,2,1,0:T(8,128)} %get-tuple-element.360, f32[2,2,4,512]{3,2,1,0:T(4,128)S(1)} %bitcast.76, f32[2,2,512,4,512]{4,2,3,1,0:T(8,128)S(1)} %get-tuple-element.437, f32[2,2,4,512]{3,2,1,0:T(4,128)S(1)} %max.5, pred[2,512,512]{1,2,0:T(8,128)(4,1)S(1)} %broadcast_compare_fusion, ...), kind=kOutput, calls=%fused_computation.7 | convolution fusion | flops 1096810496 | bytes 26279940 | tf_op jit(solution)/shard_map/while/body/eval_jaxpr/cond/branch_0_fun/shgqk,skhd->shgqd/dot_general | solution.py:105
  676.1 26.4 %convolution_convert_fusion = bf16[1024,8192]{1,0:T(8,128)(2,1)} fusion(bf16[1024,1024]{1,0:T(8,128)(2,1)} %reshape.213, bf16[1024,8192]{1,0:T(8,128)(2,1)} %all-gather.20.cloned.1.call-done), kind=kOutput, calls=%fused_computation.41 | convolution fusion | flops 17188257792 | bytes 35651584 | tf_op jit(solution)/shard_map/dot_general | solution.py:120
  702.6 152.7 %reduce-scatter.2.cloned.1.call-done = bf16[1024,2048]{1,0:T(8,128)(2,1)} async-done(((bf16[1024,8192]{1,0:T(8,128)(2,1)}), bf16[1024,2048]{1,0:T(8,128)(2,1)}) %reduce-scatter.2.cloned.1.call-update) | async-done | bytes 4194320 | tf_op jit(solution)/shard_map/reduce_scatter | solution.py:125
  (132 shorter events, 106.6 us)
Async XLA Ops:
  6.5 2.9 copy-start.1
  6.5 52.0 %all-gather.10.cloned.1.call-start = ((), (), s32[]{:S(2)}) async-start(), calls=%async_computation.2 | async-start | bytes 4718592 | tf_op jit(solution)/shard_map/all_gather | solution.py:62
  7.3 209.3 %all-gather.8.cloned.1.call-start = ((), (), s32[]{:S(2)}) async-start(), calls=%async_computation.1 | async-start | bytes 20971520 | tf_op jit(solution)/shard_map/all_gather | solution.py:50
  8.0 257.0 %all-gather.16.cloned.1.call-start = ((), (), s32[]{:S(2)}) async-start(), calls=%async_computation.5 | async-start | bytes 4718592 | tf_op jit(solution)/shard_map/all_gather | solution.py:63
  8.7 407.7 %all-gather.14.cloned.1.call-start = ((), (), s32[]{:S(2)}) async-start(), calls=%async_computation.4 | async-start | bytes 18874368 | tf_op jit(solution)/shard_map/all_gather | solution.py:61
  9.3 460.5 %all-gather.12.cloned.1.call-start = ((), (), s32[]{:S(2)}) async-start(), calls=%async_computation.3 | async-start | bytes 4718592 | tf_op jit(solution)/shard_map/all_gather | solution.py:80
  64.9 159.1 %copy-start.2 = (f32[8192]{0:T(1024)S(1)}, f32[8192]{0:T(1024)}, u32[]{:S(2)}) copy-start(f32[8192]{0:T(1024)} %param.12) | copy-start | bytes 98308
  216.5 7.5 copy-start
  234.1 276.0 %all-gather.18.cloned.1.call-start = ((), (), s32[]{:S(2)}) async-start(), calls=%async_computation.6 | async-start | bytes 4718592 | tf_op jit(solution)/shard_map/all_gather | solution.py:81
  284.1 392.1 %all-gather.20.cloned.1.call-start = ((), (), s32[]{:S(2)}) async-start(), calls=%async_computation.7 | async-start | bytes 18874368 | tf_op jit(solution)/shard_map/all_gather | solution.py:122
  284.8 570.4 %reduce-scatter.2.cloned.1.call-start = ((), (), s32[]{:S(2)}) async-start(), calls=%async_computation.8 | async-start | bytes 20971520 | tf_op jit(solution)/shard_map/reduce_scatter | solution.py:125
Sparse Core Ops, SparseCore 0:
  8.9 49.5 all-gather.9
  60.4 156.0 all-gather.7
  218.1 46.8 all-gather.15
  266.5 149.8 all-gather.13
  417.9 45.0 all-gather.11
  464.4 45.6 all-gather.17
  511.7 149.8 all-gather.19
  702.7 152.5 reduce-scatter.1
where the time goes:
time: 864 us; the launch traced here: 862 us
  waiting for transfers between devices  552 us (64%)
  matrix products  177 us (20%)
  other arithmetic  62 us (7%)
  local copies, waits for them, and re-layouts  51.1 us (6%)
  between operations  13.6 us (2%)
    reduce_scatter x1, waiting for transfers between devices, per_device(): lax.psum_scatter(terms.astype(jnp.bfloat16), 'tp', scatter_dimension=1, t...  153 us
    all_gather x1, waiting for transfers between devices, per_device(): whole = lax.all_gather(tokens, 'tp', axis=2, tiled=True)  152 us
    all_gather x1, waiting for transfers between devices, per_device(): lax.all_gather(w_query, 'ctx', axis=0, tiled=True)  131 us
    dot_general x8, matrix products, update(): jnp.einsum('shgqk,skhd->shgqd', weights.astype(jnp.bfloat16), value_block...  69.1 us
    all_gather x1, waiting for transfers between devices, per_device(): lax.all_gather(w_key, 'ctx', axis=0, tiled=True)  48 us
    dot_general x3, matrix products, per_device(): jnp.dot(normed, piece, preferred_element_type=jnp.float32)  44.1 us
    dot_general x8, matrix products, update(): jnp.einsum('shgqd,skhd->shgqk', query, key_block, preferred_element_type=...  37.6 us
    dot_general x3, local copies, waits for them, and re-layouts, per_device(): jnp.dot(normed, piece, preferred_element_type=jnp.float32)  34.1 us
  transfers between devices with their start and end apart: 8, of which 6 were waited for; matrix products, arithmetic and copies ran while one was open for 31% of the time, Pallas kernels for 0%

commit v1 on v0

--- a/solution.py
+++ b/solution.py
@@ -1,3 +1,4 @@
+import functools
 import math
 import jax
 import jax.numpy as jnp
@@ -8,6 +9,28 @@
 theta_base = 500000.0
 norm_eps = 1e-05
 masked_score = -1e30
+
+
+def shape_spans_for(packet, dim_no, axis_key):
+    odd = jax.lax.axis_size(axis_key)
+    far_arr = jax.lax.axis_index(axis_key)
+    y_new, small, formed = (odd, far_arr, packet.shape[dim_no])
+    kept_arr, v_now = (packet, 1)
+    while v_now < y_new:
+        kept_arr = jnp.concatenate(
+            [
+                kept_arr,
+                jax.lax.ppermute(
+                    kept_arr, axis_key, tuple(((m, (m - v_now) % y_new) for m in range(y_new)))
+                ),
+            ],
+            axis=dim_no,
+        )
+        v_now = 2 * v_now
+    return jnp.roll(kept_arr, small * formed, axis=dim_no)
+
+
+finish_the_cycles = functools.partial(shape_spans_for, dim_no=0, axis_key="ctx")
 
 
 def normalize(flat_rows, norm_gain):
@@ -59,7 +82,7 @@
     )
     pieces = (
         lax.all_gather(w_query, "ctx", axis=0, tiled=True),
-        lax.all_gather(w_key, "ctx", axis=0, tiled=True),
+        finish_the_cycles(w_key),
         lax.all_gather(value_weight, "ctx", axis=0, tiled=True),
     )
     query_flat, flattened_key, flattened_value = tuple(

time: 864 us -> 817 us (0.946)
  waiting for transfers between devices: 552 us -> 491 us
    all_gather x1, waiting for transfers between devices: 152 us -> 19.1 us  [per_device(): whole = lax.all_gather(tokens, 'tp', axis=2, tiled=True)]
    ppermute x0 -> x3, waiting for transfers between devices: none -> 120 us  [shape_spans_for(): jax.lax.ppermute(kept_arr, axis_key, tuple(((m, (m - v_now) % y_new) for...]
    all_gather x1 -> x0, waiting for transfers between devices: 48 us -> none  [per_device(): lax.all_gather(w_key, 'ctx', axis=0, tiled=True)]
    dot_general x3 -> x4, local copies, waits for them, and re-layouts: 34.1 us -> 36.4 us  [per_device(): jnp.dot(normed, piece, preferred_element_type=jnp.float32)]
  transfers between devices with their start and end apart: 8 -> 10, of which waited for: 6 -> 8; matrix products, arithmetic and copies ran while one was open for 31% -> 33% of each run, Pallas kernels for 0% -> 0%
where the time goes in v1:
time: 817 us; the launch traced here: 814 us
  waiting for transfers between devices  491 us (60%)
  matrix products  177 us (22%)
  other arithmetic  65.3 us (8%)
  local copies, waits for them, and re-layouts  56.2 us (7%)
  between operations  13.7 us (2%)
    reduce_scatter x1, waiting for transfers between devices, per_device(): lax.psum_scatter(terms.astype(jnp.bfloat16), 'tp', scatter_dimension=1, t...  153 us
    all_gather x1, waiting for transfers between devices, per_device(): lax.all_gather(w_query, 'ctx', axis=0, tiled=True)  132 us
    ppermute x3, waiting for transfers between devices, shape_spans_for(): jax.lax.ppermute(kept_arr, axis_key, tuple(((m, (m - v_now) % y_new) for...  120 us
    dot_general x8, matrix products, update(): jnp.einsum('shgqk,skhd->shgqd', weights.astype(jnp.bfloat16), value_block...  69.1 us
    dot_general x3, matrix products, per_device(): jnp.dot(normed, piece, preferred_element_type=jnp.float32)  44.1 us
    dot_general x8, matrix products, update(): jnp.einsum('shgqd,skhd->shgqk', query, key_block, preferred_element_type=...  37.5 us
    dot_general x4, local copies, waits for them, and re-layouts, per_device(): jnp.dot(normed, piece, preferred_element_type=jnp.float32)  36.4 us
    all_gather x1, waiting for transfers between devices, per_device(): value_piece = lax.all_gather(own_values, 'ctx', axis=1, tiled=True)  33.8 us
  transfers between devices with their start and end apart: 10, of which 8 were waited for; matrix products, arithmetic and copies ran while one was open for 33% of the time, Pallas kernels for 0%

profile of v1, /device:TPU:0, one launch (start us, length us, event | category | flops | bytes accessed | tf_op | source)
XLA Modules:
  0.0 814.2 jit_solution(12348866576866406472)
XLA Ops:
  13.4 7.0 collective-permute-done
  22.4 23.2 %collective-permute-done.1 = bf16[2048,256]{1,0:T(8,128)(2,1)S(1)} collective-permute-done((bf16[2048,256]{1,0:T(8,128)(2,1)S(1)}, bf16[2048,256]{1,0:T(8,128)(2,1)S(1)}, u32[]{:S(2)}, u32[]{:S(2)}) %collective-permute-start.1) | collective-permute-done | bytes 1048608 | tf_op jit(solution)/shard_map/ppermute | solution.py:23
  51.3 89.7 %collective-permute-done.2 = bf16[4096,256]{1,0:T(8,128)(2,1)S(1)} collective-permute-done((bf16[4096,256]{1,0:T(8,128)(2,1)}, bf16[4096,256]{1,0:T(8,128)(2,1)S(1)}, u32[]{:S(2)}, u32[]{:S(2)}) %collective-permute-start.2) | collective-permute-done | bytes 2097184 | tf_op jit(solution)/shard_map/ppermute | solution.py:23
  150.1 19.1 %all-gather.7.cloned.1.call-done = bf16[2,512,8192]{2,1,0:T(8,128)(2,1)} async-done(((bf16[2,512,2048]{2,1,0:T(8,128)(2,1)}), bf16[2,512,8192]{2,1,0:T(8,128)(2,1)}) %all-gather.7.cloned.1.call-update) | async-done | bytes 16777232 | tf_op jit(solution)/shard_map/all_gather | solution.py:73
  169.2 7.5 fusion.21
  176.7 9.0 %fusion.29 = f32[2,512,2,128]{1,3,2,0:T(8,128)S(1)} fusion(bf16[2,128,8192,1]{2,1,0,3:T(8,128)(2,1)S(1)} %bitcast.69, bf16[2,512,8192]{2,1,0:T(8,128)(2,1)} %all-gather.7.cloned.1.call-done, f32[8192]{0:T(1024)S(1)} %copy-done.7, f32[2,512]{1,0:T(2,128)S(1)} %add_rsqrt_fusion), kind=kOutput, calls=%fused_computation.52 | convolution fusion | flops 4328521728 | bytes 22056960 | tf_op jit(solution)/shard_map/dot_general | solution.py:89
  187.0 30.8 %all-gather.13.cloned.1.call-done = bf16[8192,256]{1,0:T(8,128)(2,1)} async-done(((bf16[1024,256]{1,0:T(8,128)(2,1)}), bf16[8192,256]{1,0:T(8,128)(2,1)}) %all-gather.13.cloned.1.call-update) | async-done | bytes 4194320 | tf_op jit(solution)/shard_map/all_gather | solution.py:86
  224.1 12.7 %convolution_convert_fusion.1 = bf16[2,512,2,128]{3,1,2,0:T(8,128)(2,1)} fusion(bf16[2,128,8192,1]{2,1,0,3:T(8,128)(2,1)} %bitcast.70, bf16[2,512,8192]{2,1,0:T(8,128)(2,1)} %all-gather.7.cloned.1.call-done, f32[8192]{0:T(1024)S(1)} %copy-done.7, f32[2,512]{1,0:T(2,128)S(1)} %add_rsqrt_fusion), kind=kOutput, calls=%fused_computation.49 | convolution fusion | flops 4328783872 | bytes 21532672 | tf_op jit(solution)/shard_map/dot_general | solution.py:89
  237.8 131.5 %all-gather.11.cloned.1.call-done = bf16[8192,1024]{1,0:T(8,128)(2,1)} async-done(((bf16[1024,1024]{1,0:T(8,128)(2,1)}), bf16[8192,1024]{1,0:T(8,128)(2,1)}) %all-gather.11.cloned.1.call-update) | async-done | bytes 16777232 | tf_op jit(solution)/shard_map/all_gather | solution.py:84
  369.3 21.5 %copy.25 = bf16[1024,8192]{1,0:T(8,128)(2,1)} copy(bf16[1024,8192]{0,1:T(8,128)(2,1)} %bitcast.64) | data formatting | bytes 33554432 | tf_op jit(solution)/shard_map/dot_general | solution.py:89
  390.8 22.4 %fusion.27 = f32[2,512,8,128]{1,3,2,0:T(8,128)S(1)} fusion(bf16[8,128,8192,1]{2,1,0,3:T(8,128)(2,1)} %bitcast.65, bf16[2,512,8192]{2,1,0:T(8,128)(2,1)} %all-gather.7.cloned.1.call-done, f32[8192]{0:T(1024)S(1)} %copy-done.7, f32[2,512]{1,0:T(2,128)S(1)} %add_rsqrt_fusion), kind=kOutput, calls=%fused_computation.51 | convolution fusion | flops 17213423616 | bytes 37785600 | tf_op jit(solution)/shard_map/dot_general | solution.py:89
  422.8 6.4 copy.29
  429.2 33.8 %all-gather.15.cloned.1.call-done = bf16[2,4096,2,128]{3,1,2,0:T(8,128)(2,1)} async-done(((bf16[2,512,2,128]{3,1,2,0:T(8,128)(2,1)}), bf16[2,4096,2,128]{3,1,2,0:T(8,128)(2,1)}) %all-gather.15.cloned.1.call-update) | async-done | bytes 4194320 | tf_op jit(solution)/shard_map/all_gather | solution.py:104
  465.4 155.1 %while.19 = (s32[]{:T(128)}, f32[2,2,4,512]{3,2,1,0:T(4,128)S(1)}, f32[2,2,4,512]{3,2,1,0:T(4,128)S(1)}, f32[2,2,4,512,128]{4,3,2,1,0:T(8,128)}, s32[2,16]{1,0:T...) while((s32[]{:T(128)}, f32[2,2,4,512]{3,2,1,0:T(4,128)S(1)}, ...), condition=%wide.region_11.12_spmd, body=%wide.region_3.11_spmd.sunk | while | flops 2204700672 | bytes 64532936 | solution.py:140
  467.0 17.9 %conditional.2 = (f32[2,2,4,512]{3,2,1,0:T(4,128)S(1)}, f32[2,2,4,512]{3,2,1,0:T(4,128)S(1)}, f32[2,2,4,512,128]{4,3,2,1,0:T(8,128)}) conditional(s32[]{:T(128)} %convert_element_type.85, (s32[2,512]{1,0:T(2,128)S(1)}, s32[2,512]{1,0:T(2,128)S(1)}, s32[]{:T(128)}, bf16[2,4096,2,128]{3,1,2,0:T(8,128)(2,1)}, bf16[2,2,4,512,128]{4,3,2,1,0:T(8,128)(2,1)}, ...), branch_computations={%region_7.9_spmd, %region_10.10_spmd} | conditional | flops 2204647424 | bytes 64430148 | solution.py:136
  476.2 8.7 %multiply_add_fusion = f32[2,2,4,512,128]{4,3,2,1,0:T(8,128)} fusion(f32[2,2,4,512,128]{4,3,2,1,0:T(8,128)} %get-tuple-element.360, f32[2,2,4,512]{3,2,1,0:T(4,128)S(1)} %bitcast.76, f32[2,2,512,4,512]{4,2,3,1,0:T(8,128)S(1)} %get-tuple-element.437, f32[2,2,4,512]{3,2,1,0:T(4,128)S(1)} %max.5, pred[2,512,512]{1,2,0:T(8,128)(4,1)S(1)} %broadcast_compare_fusion, ...), kind=kOutput, calls=%fused_computation.7 | convolution fusion | flops 1096810496 | bytes 26279940 | tf_op jit(solution)/shard_map/while/body/eval_jaxpr/cond/branch_0_fun/shgqk,skhd->shgqd/dot_general | solution.py:128
  486.4 17.9 %conditional.2 = (f32[2,2,4,512]{3,2,1,0:T(4,128)S(1)}, f32[2,2,4,512]{3,2,1,0:T(4,128)S(1)}, f32[2,2,4,512,128]{4,3,2,1,0:T(8,128)}) conditional(s32[]{:T(128)} %convert_element_type.85, (s32[2,512]{1,0:T(2,128)S(1)}, s32[2,512]{1,0:T(2,128)S(1)}, s32[]{:T(128)}, bf16[2,4096,2,128]{3,1,2,0:T(8,128)(2,1)}, bf16[2,2,4,512,128]{4,3,2,1,0:T(8,128)(2,1)}, ...), branch_computations={%region_7.9_spmd, %region_10.10_spmd} | conditional | flops 2204647424 | bytes 64430148 | solution.py:136
  495.6 8.7 %multiply_add_fusion = f32[2,2,4,512,128]{4,3,2,1,0:T(8,128)} fusion(f32[2,2,4,512,128]{4,3,2,1,0:T(8,128)} %get-tuple-element.360, f32[2,2,4,512]{3,2,1,0:T(4,128)S(1)} %bitcast.76, f32[2,2,512,4,512]{4,2,3,1,0:T(8,128)S(1)} %get-tuple-element.437, f32[2,2,4,512]{3,2,1,0:T(4,128)S(1)} %max.5, pred[2,512,512]{1,2,0:T(8,128)(4,1)S(1)} %broadcast_compare_fusion, ...), kind=kOutput, calls=%fused_computation.7 | convolution fusion | flops 1096810496 | bytes 26279940 | tf_op jit(solution)/shard_map/while/body/eval_jaxpr/cond/branch_0_fun/shgqk,skhd->shgqd/dot_general | solution.py:128
  505.8 17.8 %conditional.2 = (f32[2,2,4,512]{3,2,1,0:T(4,128)S(1)}, f32[2,2,4,512]{3,2,1,0:T(4,128)S(1)}, f32[2,2,4,512,128]{4,3,2,1,0:T(8,128)}) conditional(s32[]{:T(128)} %convert_element_type.85, (s32[2,512]{1,0:T(2,128)S(1)}, s32[2,512]{1,0:T(2,128)S(1)}, s32[]{:T(128)}, bf16[2,4096,2,128]{3,1,2,0:T(8,128)(2,1)}, bf16[2,2,4,512,128]{4,3,2,1,0:T(8,128)(2,1)}, ...), branch_computations={%region_7.9_spmd, %region_10.10_spmd} | conditional | flops 2204647424 | bytes 64430148 | solution.py:136
  515.0 8.6 %multiply_add_fusion = f32[2,2,4,512,128]{4,3,2,1,0:T(8,128)} fusion(f32[2,2,4,512,128]{4,3,2,1,0:T(8,128)} %get-tuple-element.360, f32[2,2,4,512]{3,2,1,0:T(4,128)S(1)} %bitcast.76, f32[2,2,512,4,512]{4,2,3,1,0:T(8,128)S(1)} %get-tuple-element.437, f32[2,2,4,512]{3,2,1,0:T(4,128)S(1)} %max.5, pred[2,512,512]{1,2,0:T(8,128)(4,1)S(1)} %broadcast_compare_fusion, ...), kind=kOutput, calls=%fused_computation.7 | convolution fusion | flops 1096810496 | bytes 26279940 | tf_op jit(solution)/shard_map/while/body/eval_jaxpr/cond/branch_0_fun/shgqk,skhd->shgqd/dot_general | solution.py:128
  525.2 18.0 %conditional.2 = (f32[2,2,4,512]{3,2,1,0:T(4,128)S(1)}, f32[2,2,4,512]{3,2,1,0:T(4,128)S(1)}, f32[2,2,4,512,128]{4,3,2,1,0:T(8,128)}) conditional(s32[]{:T(128)} %convert_element_type.85, (s32[2,512]{1,0:T(2,128)S(1)}, s32[2,512]{1,0:T(2,128)S(1)}, s32[]{:T(128)}, bf16[2,4096,2,128]{3,1,2,0:T(8,128)(2,1)}, bf16[2,2,4,512,128]{4,3,2,1,0:T(8,128)(2,1)}, ...), branch_computations={%region_7.9_spmd, %region_10.10_spmd} | conditional | flops 2204647424 | bytes 64430148 | solution.py:136
  534.4 8.7 %multiply_add_fusion = f32[2,2,4,512,128]{4,3,2,1,0:T(8,128)} fusion(f32[2,2,4,512,128]{4,3,2,1,0:T(8,128)} %get-tuple-element.360, f32[2,2,4,512]{3,2,1,0:T(4,128)S(1)} %bitcast.76, f32[2,2,512,4,512]{4,2,3,1,0:T(8,128)S(1)} %get-tuple-element.437, f32[2,2,4,512]{3,2,1,0:T(4,128)S(1)} %max.5, pred[2,512,512]{1,2,0:T(8,128)(4,1)S(1)} %broadcast_compare_fusion, ...), kind=kOutput, calls=%fused_computation.7 | convolution fusion | flops 1096810496 | bytes 26279940 | tf_op jit(solution)/shard_map/while/body/eval_jaxpr/cond/branch_0_fun/shgqk,skhd->shgqd/dot_general | solution.py:128
  544.6 17.8 %conditional.2 = (f32[2,2,4,512]{3,2,1,0:T(4,128)S(1)}, f32[2,2,4,512]{3,2,1,0:T(4,128)S(1)}, f32[2,2,4,512,128]{4,3,2,1,0:T(8,128)}) conditional(s32[]{:T(128)} %convert_element_type.85, (s32[2,512]{1,0:T(2,128)S(1)}, s32[2,512]{1,0:T(2,128)S(1)}, s32[]{:T(128)}, bf16[2,4096,2,128]{3,1,2,0:T(8,128)(2,1)}, bf16[2,2,4,512,128]{4,3,2,1,0:T(8,128)(2,1)}, ...), branch_computations={%region_7.9_spmd, %region_10.10_spmd} | conditional | flops 2204647424 | bytes 64430148 | solution.py:136
  553.9 8.6 %multiply_add_fusion = f32[2,2,4,512,128]{4,3,2,1,0:T(8,128)} fusion(f32[2,2,4,512,128]{4,3,2,1,0:T(8,128)} %get-tuple-element.360, f32[2,2,4,512]{3,2,1,0:T(4,128)S(1)} %bitcast.76, f32[2,2,512,4,512]{4,2,3,1,0:T(8,128)S(1)} %get-tuple-element.437, f32[2,2,4,512]{3,2,1,0:T(4,128)S(1)} %max.5, pred[2,512,512]{1,2,0:T(8,128)(4,1)S(1)} %broadcast_compare_fusion, ...), kind=kOutput, calls=%fused_computation.7 | convolution fusion | flops 1096810496 | bytes 26279940 | tf_op jit(solution)/shard_map/while/body/eval_jaxpr/cond/branch_0_fun/shgqk,skhd->shgqd/dot_general | solution.py:128
  564.0 17.8 %conditional.2 = (f32[2,2,4,512]{3,2,1,0:T(4,128)S(1)}, f32[2,2,4,512]{3,2,1,0:T(4,128)S(1)}, f32[2,2,4,512,128]{4,3,2,1,0:T(8,128)}) conditional(s32[]{:T(128)} %convert_element_type.85, (s32[2,512]{1,0:T(2,128)S(1)}, s32[2,512]{1,0:T(2,128)S(1)}, s32[]{:T(128)}, bf16[2,4096,2,128]{3,1,2,0:T(8,128)(2,1)}, bf16[2,2,4,512,128]{4,3,2,1,0:T(8,128)(2,1)}, ...), branch_computations={%region_7.9_spmd, %region_10.10_spmd} | conditional | flops 2204647424 | bytes 64430148 | solution.py:136
  573.2 8.6 %multiply_add_fusion = f32[2,2,4,512,128]{4,3,2,1,0:T(8,128)} fusion(f32[2,2,4,512,128]{4,3,2,1,0:T(8,128)} %get-tuple-element.360, f32[2,2,4,512]{3,2,1,0:T(4,128)S(1)} %bitcast.76, f32[2,2,512,4,512]{4,2,3,1,0:T(8,128)S(1)} %get-tuple-element.437, f32[2,2,4,512]{3,2,1,0:T(4,128)S(1)} %max.5, pred[2,512,512]{1,2,0:T(8,128)(4,1)S(1)} %broadcast_compare_fusion, ...), kind=kOutput, calls=%fused_computation.7 | convolution fusion | flops 1096810496 | bytes 26279940 | tf_op jit(solution)/shard_map/while/body/eval_jaxpr/cond/branch_0_fun/shgqk,skhd->shgqd/dot_general | solution.py:128
  583.3 17.8 %conditional.2 = (f32[2,2,4,512]{3,2,1,0:T(4,128)S(1)}, f32[2,2,4,512]{3,2,1,0:T(4,128)S(1)}, f32[2,2,4,512,128]{4,3,2,1,0:T(8,128)}) conditional(s32[]{:T(128)} %convert_element_type.85, (s32[2,512]{1,0:T(2,128)S(1)}, s32[2,512]{1,0:T(2,128)S(1)}, s32[]{:T(128)}, bf16[2,4096,2,128]{3,1,2,0:T(8,128)(2,1)}, bf16[2,2,4,512,128]{4,3,2,1,0:T(8,128)(2,1)}, ...), branch_computations={%region_7.9_spmd, %region_10.10_spmd} | conditional | flops 2204647424 | bytes 64430148 | solution.py:136
  592.6 8.6 %multiply_add_fusion = f32[2,2,4,512,128]{4,3,2,1,0:T(8,128)} fusion(f32[2,2,4,512,128]{4,3,2,1,0:T(8,128)} %get-tuple-element.360, f32[2,2,4,512]{3,2,1,0:T(4,128)S(1)} %bitcast.76, f32[2,2,512,4,512]{4,2,3,1,0:T(8,128)S(1)} %get-tuple-element.437, f32[2,2,4,512]{3,2,1,0:T(4,128)S(1)} %max.5, pred[2,512,512]{1,2,0:T(8,128)(4,1)S(1)} %broadcast_compare_fusion, ...), kind=kOutput, calls=%fused_computation.7 | convolution fusion | flops 1096810496 | bytes 26279940 | tf_op jit(solution)/shard_map/while/body/eval_jaxpr/cond/branch_0_fun/shgqk,skhd->shgqd/dot_general | solution.py:128
  602.7 17.8 %conditional.2 = (f32[2,2,4,512]{3,2,1,0:T(4,128)S(1)}, f32[2,2,4,512]{3,2,1,0:T(4,128)S(1)}, f32[2,2,4,512,128]{4,3,2,1,0:T(8,128)}) conditional(s32[]{:T(128)} %convert_element_type.85, (s32[2,512]{1,0:T(2,128)S(1)}, s32[2,512]{1,0:T(2,128)S(1)}, s32[]{:T(128)}, bf16[2,4096,2,128]{3,1,2,0:T(8,128)(2,1)}, bf16[2,2,4,512,128]{4,3,2,1,0:T(8,128)(2,1)}, ...), branch_computations={%region_7.9_spmd, %region_10.10_spmd} | conditional | flops 2204647424 | bytes 64430148 | solution.py:136
  611.9 8.6 %multiply_add_fusion = f32[2,2,4,512,128]{4,3,2,1,0:T(8,128)} fusion(f32[2,2,4,512,128]{4,3,2,1,0:T(8,128)} %get-tuple-element.360, f32[2,2,4,512]{3,2,1,0:T(4,128)S(1)} %bitcast.76, f32[2,2,512,4,512]{4,2,3,1,0:T(8,128)S(1)} %get-tuple-element.437, f32[2,2,4,512]{3,2,1,0:T(4,128)S(1)} %max.5, pred[2,512,512]{1,2,0:T(8,128)(4,1)S(1)} %broadcast_compare_fusion, ...), kind=kOutput, calls=%fused_computation.7 | convolution fusion | flops 1096810496 | bytes 26279940 | tf_op jit(solution)/shard_map/while/body/eval_jaxpr/cond/branch_0_fun/shgqk,skhd->shgqd/dot_general | solution.py:128
  627.9 26.4 %convolution_convert_fusion = bf16[1024,8192]{1,0:T(8,128)(2,1)} fusion(bf16[1024,1024]{1,0:T(8,128)(2,1)} %reshape.213, bf16[1024,8192]{1,0:T(8,128)(2,1)} %all-gather.17.cloned.1.call-done), kind=kOutput, calls=%fused_computation.41 | convolution fusion | flops 17188257792 | bytes 35651584 | tf_op jit(solution)/shard_map/dot_general | solution.py:143
  654.4 153.0 %reduce-scatter.2.cloned.1.call-done = bf16[1024,2048]{1,0:T(8,128)(2,1)} async-done(((bf16[1024,8192]{1,0:T(8,128)(2,1)}), bf16[1024,2048]{1,0:T(8,128)(2,1)}) %reduce-scatter.2.cloned.1.call-update) | async-done | bytes 4194320 | tf_op jit(solution)/shard_map/reduce_scatter | solution.py:148
  (156 shorter events, 131.9 us)
Async XLA Ops:
  6.5 39.1 %copy-start = (bf16[1024,256]{1,0:T(8,128)(2,1)S(1)}, bf16[1024,256]{1,0:T(8,128)(2,1)}, u32[]{:S(2)}) copy-start(bf16[1024,256]{1,0:T(8,128)(2,1)} %param.15) | copy-start | bytes 1572868
  6.5 40.6 %copy-start.6 = (s32[2,16]{1,0:T(2,128)S(1)}, s32[2,16]{1,0:T(2,128)}, u32[]{:S(2)}) copy-start(s32[2,16]{1,0:T(2,128)} %param.13) | copy-start | bytes 388
  6.5 162.7 %all-gather.7.cloned.1.call-start = ((), (), s32[]{:S(2)}) async-start(), calls=%async_computation.1 | async-start | bytes 20971520 | tf_op jit(solution)/shard_map/all_gather | solution.py:73
  7.3 210.5 %all-gather.13.cloned.1.call-start = ((), (), s32[]{:S(2)}) async-start(), calls=%async_computation.4 | async-start | bytes 4718592 | tf_op jit(solution)/shard_map/all_gather | solution.py:86
  8.0 361.3 %all-gather.11.cloned.1.call-start = ((), (), s32[]{:S(2)}) async-start(), calls=%async_computation.3 | async-start | bytes 18874368 | tf_op jit(solution)/shard_map/all_gather | solution.py:84
  8.7 414.0 %all-gather.9.cloned.1.call-start = ((), (), s32[]{:S(2)}) async-start(), calls=%async_computation.2 | async-start | bytes 4718592 | tf_op jit(solution)/shard_map/all_gather | solution.py:103
  8.8 11.6 %collective-permute-start = (bf16[1024,256]{1,0:T(8,128)(2,1)}, bf16[1024,256]{1,0:T(8,128)(2,1)S(1)}, u32[]{:S(2)}, u32[]{:S(2)}) collective-permute-start(bf16[1024,256]{1,0:T(8,128)(2,1)} %param.15), channel_id=1, source_target_pairs={{0,28},{4,0},{8,4},{12,8},{16,12},{20,16},{24,20},{28,24},{1,29},{... | collective-permute-start | bytes 1572872 | tf_op jit(solution)/shard_map/ppermute | solution.py:23
  20.4 26.7 %copy-start.2 = (bf16[1024,256]{1,0:T(8,128)(2,1)}, bf16[1024,256]{1,0:T(8,128)(2,1)S(1)}, u32[]{:S(2)}) copy-start(bf16[1024,256]{1,0:T(8,128)(2,1)S(1)} %collective-permute-done) | copy-start | bytes 1572868
  21.8 23.7 %collective-permute-start.1 = (bf16[2048,256]{1,0:T(8,128)(2,1)S(1)}, bf16[2048,256]{1,0:T(8,128)(2,1)S(1)}, u32[]{:S(2)}, u32[]{:S(2)}) collective-permute-start(bf16[2048,256]{1,0:T(8,128)(2,1)S(1)} %pad_maximum_fusion.1), channel_id=1, source_target_pairs={{0,24},{4,28},{8,0},{12,4},{16,8},{20,12},{24,16},{28,20},{1,25},{... | collective-permute-start | bytes 3145736 | tf_op jit(solution)/shard_map/ppermute | solution.py:23
  47.1 94.0 %collective-permute-start.2 = (bf16[4096,256]{1,0:T(8,128)(2,1)}, bf16[4096,256]{1,0:T(8,128)(2,1)S(1)}, u32[]{:S(2)}, u32[]{:S(2)}) collective-permute-start(bf16[4096,256]{1,0:T(8,128)(2,1)} %pad_maximum_fusion), channel_id=1, source_target_pairs={{0,16},{4,20},{8,24},{12,28},{16,0},{20,4},{24,8},{28,12},{1,17},{... | collective-permute-start | bytes 6291464 | tf_op jit(solution)/shard_map/ppermute | solution.py:23
  47.1 94.1 %copy-start.1 = (bf16[1024,256]{1,0:T(8,128)(2,1)S(1)}, bf16[1024,256]{1,0:T(8,128)(2,1)}, u32[]{:S(2)}) copy-start(bf16[1024,256]{1,0:T(8,128)(2,1)} %param.15) | copy-start | bytes 1572868
  47.1 94.1 %copy-start.3 = (bf16[1024,256]{1,0:T(8,128)(2,1)S(1)}, bf16[1024,256]{1,0:T(8,128)(2,1)}, u32[]{:S(2)}) copy-start(bf16[1024,256]{1,0:T(8,128)(2,1)} %copy-done.2) | copy-start | bytes 1572868
  150.1 26.6 %copy-start.7 = (f32[8192]{0:T(1024)S(1)}, f32[8192]{0:T(1024)}, u32[]{:S(2)}) copy-start(f32[8192]{0:T(1024)} %param.12) | copy-start | bytes 98308
  169.2 7.5 copy-start.4
  176.7 9.1 %copy-start.5 = (f32[2,512,64]{1,2,0:T(8,128)S(1)}, f32[2,512,64]{1,2,0:T(8,128)}, u32[]{:S(2)}) copy-start(f32[2,512,64]{1,2,0:T(8,128)} %get-tuple-element.445) | copy-start | bytes 786436
  186.9 276.1 %all-gather.15.cloned.1.call-start = ((), (), s32[]{:S(2)}) async-start(), calls=%async_computation.5 | async-start | bytes 4718592 | tf_op jit(solution)/shard_map/all_gather | solution.py:104
  236.8 391.1 %all-gather.17.cloned.1.call-start = ((), (), s32[]{:S(2)}) async-start(), calls=%async_computation.6 | async-start | bytes 18874368 | tf_op jit(solution)/shard_map/all_gather | solution.py:145
  237.4 569.9 %reduce-scatter.2.cloned.1.call-start = ((), (), s32[]{:S(2)}) async-start(), calls=%async_computation.7 | async-start | bytes 20971520 | tf_op jit(solution)/shard_map/reduce_scatter | solution.py:148
Sparse Core Ops, SparseCore 0:
  9.2 160.0 all-gather.6
  170.8 46.8 all-gather.12
  219.4 149.8 all-gather.10
  370.7 45.0 all-gather.8
  417.3 45.6 all-gather.14
  464.4 149.8 all-gather.16
  654.5 152.8 reduce-scatter.1
